TPU v7x, 32 devices: a whole 2x2x4 slice. The times are simulated.
32 devices in a mesh: shot: 2 (over y), gx: 4 (over z), gy: 4 (over x, core).
Axes of the slice: x: 2, y: 2, z: 4, core: 2. Of those that a mesh axis runs over, the one named last changes fastest.
Arguments:
- wavefield: float32 [9, 64, 64, 128], P(None, ('shot', 'gx'), 'gy'), parts along dimension 1, may hold values from -10 to 10
- labels: int32 [32, 64, 128], P('gx', 'gy'), may hold values from 0 to 7
- lame_table: float32 [8], replicated, may hold values from 0.5 to 2
- shear_table: float32 [8], replicated, may hold values from 0.1 to 0.6
- density_table: float32 [8], replicated, may hold values from 0.8 to 2
- source_cells: int32 [128], P('shot'), parts along dimension 0, may hold values from 0 to 262143
- source_amps: float32 [5, 128], P(None, 'shot'), parts along dimension 1, may hold values from -6 to 6
- receiver_cells: int32 [256], replicated, may hold values from 0 to 262143
Outputs:
- final_fields: float32 [9, 64, 64, 128], P(None, ('shot', 'gx'), 'gy'), parts along dimension 1
- traces: float32 [5, 512], P(None, 'shot'), parts along dimension 1
There are 2 independent parts, one for each index of `shot`. A program takes and returns all parts, laid end to end along the dimension named above; an argument that names none is the same for every part. Nothing has to cross between parts.
Inputs may be any that keep to these rules, and one draw needn't show every extreme that they name: `source_cells`: a flat cell index, x slowest, z fastest. `receiver_cells`: a flat cell index, x slowest, z fastest.
All inputs are finite; a program needn't handle non-finite values.
Results may differ from a plain program's by a relative error of at most 0.00002.
Values sent between devices are 32-bit elements; how exact they have to be, the bound alone decides.
A program may use at most 64 MiB of HBM per device.

v0:
```python
import functools

import jax
import jax.numpy as jnp
from jax import lax
from jax.experimental import pallas as pl
from jax.experimental.pallas import tpu as pltpu
from jax.sharding import PartitionSpec as P

coeffs = (1225.0 / 1024.0, -245.0 / 3072.0, 49.0 / 5120.0, -5.0 / 7168.0)
time_step = 0.15
sponge_width = 16.0

VX, VY, VZ, SXX, SYY, SZZ, SXY, SXZ, SYZ = range(9)
EXCHANGED = {
    (SXY, 0): False, (SXX, 0): True, (SXZ, 0): False,
    (SYY, 1): True, (SXY, 1): False, (SYZ, 1): False,
    (VY, 0): True, (VX, 0): False, (VZ, 0): True,
    (VX, 1): True, (VY, 1): False, (VZ, 1): True,
}
SLOT = {key: number for number, key in enumerate(EXCHANGED)}
RIM_X = 4
RIM_Y = 8
EXACT = lax.Precision.HIGHEST


def quotient(value, count):
    if count & (count - 1) == 0:
        return lax.shift_right_logical(value, jnp.full(value.shape, count.bit_length() - 1, value.dtype))
    return lax.div(value, jnp.full(value.shape, count, value.dtype))


def remainder(value, count):
    if count & (count - 1) == 0:
        return value & (count - 1)
    return value - quotient(value, count) * count


def profile(position, count):
    distance = jnp.minimum(position, count - 1 - position).astype(jnp.float32)
    depth = jnp.maximum(sponge_width - distance, 0.0) / sponge_width
    return jnp.exp(-(0.5 * depth) * (0.5 * depth))


def kernel(
    sizes,
    wave_ref, labels_ref, lame_ref, shear_ref, density_ref,
    source_ref, amps_ref, probe_ref,
    out_ref, traces_ref,
    F, labels, lame, shear, buoy, damp, bands, source_z, probe_z, probe_row, push, press,
    rows_y, rows_x,
    load_sem, send_sem, recv_sem, tsend_y, trecv_y, tsend_x, trecv_x,
):
    nx, ny, steps = sizes
    _, wx, wy, nz = wave_ref.shape
    gx, gy = lax.axis_index("gx"), lax.axis_index("gy")
    place = (gx, gy)
    extent = (nx, ny)
    axis_name = ("gx", "gy")
    LX, LY = slice(RIM_X, RIM_X + wx), slice(RIM_Y, RIM_Y + wy)

    def local(f):
        return F.at[f, LX, LY, :]

    loads = [
        pltpu.make_async_copy(wave_ref.at[f], local(f), load_sem.at[f]) for f in range(9)
    ]
    load_labels = pltpu.make_async_copy(labels_ref, labels, load_sem.at[9])
    for f in (SXY, SXX, SXZ, SYY, SYZ):
        loads[f].start()
    load_labels.start()
    for f in (SZZ, VY, VX, VZ):
        loads[f].start()

    for f, axis in EXCHANGED:
        if axis == 0:
            F[f, :RIM_X, LY, :] = jnp.zeros((RIM_X, wy, nz), jnp.float32)
            F[f, RIM_X + wx :, LY, :] = jnp.zeros((RIM_X, wy, nz), jnp.float32)
        else:
            F[f, LX, :RIM_Y, :] = jnp.zeros((wx, RIM_Y, nz), jnp.float32)
            F[f, LX, RIM_Y + wy :, :] = jnp.zeros((wx, RIM_Y, nz), jnp.float32)
    rows_y[...] = jnp.zeros(rows_y.shape, jnp.float32)

    barrier = pltpu.get_barrier_semaphore()
    for axis in (0, 1):
        for d in range(1, extent[axis]):
            pl.semaphore_signal(
                barrier, inc=1,
                device_id={axis_name[axis]: lax.rem(place[axis] + d, extent[axis])},
                device_id_type=pl.DeviceIdType.MESH,
            )
    pl.semaphore_wait(barrier, nx + ny - 2)

    def copy(f, axis, up):
        forward = EXCHANGED[f, axis]
        n = extent[axis]
        target = lax.rem(place[axis] + (1 if up else n - 1), n)
        if axis == 0:
            count = 3 if forward == up else 4
            if up:
                src, dst = RIM_X + wx - count, RIM_X - count
            else:
                src, dst = RIM_X, RIM_X + wx
            source = F.at[f, src : src + count, LY, :]
            sink = F.at[f, dst : dst + count, LY, :]
        else:
            src, dst = (wy, 0) if up else (RIM_Y, RIM_Y + wy)
            source = F.at[f, LX, src : src + RIM_Y, :]
            sink = F.at[f, LX, dst : dst + RIM_Y, :]
        slot = SLOT[f, axis]
        return pltpu.make_async_remote_copy(
            src_ref=source, dst_ref=sink,
            send_sem=send_sem.at[slot, int(up)], recv_sem=recv_sem.at[slot, int(up)],
            device_id={axis_name[axis]: target}, device_id_type=pl.DeviceIdType.MESH,
        )

    has_low = (gx > 0, gy > 0)
    has_high = (gx < nx - 1, gy < ny - 1)

    def send(*keys):
        for f, axis in keys:
            @pl.when(has_high[axis])
            def _():
                copy(f, axis, True).start()

            @pl.when(has_low[axis])
            def _():
                copy(f, axis, False).start()

    def sent(*keys):
        for axis in (0, 1):
            mine = [f for f, a in keys if a == axis]

            @pl.when(has_high[axis])
            def _():
                for f in mine:
                    copy(f, axis, True).wait_send()

            @pl.when(has_low[axis])
            def _():
                for f in mine:
                    copy(f, axis, False).wait_send()

    def arrived(*keys):
        for f, axis in keys:
            @pl.when(has_low[axis])
            def _():
                copy(f, axis, True).wait_recv()

            @pl.when(has_high[axis])
            def _():
                copy(f, axis, False).wait_recv()

    def tap(f, axis, offset):
        if axis == 0:
            return F[f, RIM_X + offset : RIM_X + offset + wx, LY, :]
        return F[f, LX, RIM_Y + offset : RIM_Y + offset + wy, :]

    def along(f, axis):
        forward = EXCHANGED[f, axis]
        result = None
        for k in range(1, 5):
            later, earlier = (k, 1 - k) if forward else (k - 1, -k)
            term = coeffs[k - 1] * (tap(f, axis, later) - tap(f, axis, earlier))
            result = term if result is None else result + term
        return result

    def depth(f, forward):
        flat = F[f, LX, LY, :].reshape(wx * wy, nz)
        return jnp.dot(
            flat, bands[int(forward)], precision=EXACT, preferred_element_type=jnp.float32
        ).reshape(wx, wy, nz)

    stress_keys = [(SXY, 0), (SYY, 1), (SXX, 0), (SXY, 1), (SXZ, 0), (SYZ, 1)]
    speed_keys = [(VY, 0), (VX, 1), (VX, 0), (VY, 1), (VZ, 0), (VZ, 1)]

    for f in (SXY, SYY, SXX, SXZ, SYZ):
        loads[f].wait()
    send(*stress_keys)

    load_labels.wait()
    tissue = labels[...]

    def lookup(table):
        value = jnp.zeros(tissue.shape, jnp.float32)
        for number in range(table.shape[0]):
            value = jnp.where(tissue == number, table[number], value)
        return value

    lame[...] = time_step * lookup(lame_ref)
    shear[...] = time_step * lookup(shear_ref)
    buoy[...] = time_step / lookup(density_ref)
    shape = (wx, wy, nz)
    damp[...] = (
        profile(gx * wx + lax.broadcasted_iota(jnp.int32, shape, 0), nx * wx)
        * profile(gy * wy + lax.broadcasted_iota(jnp.int32, shape, 1), ny * wy)
        * profile(lax.broadcasted_iota(jnp.int32, shape, 2), nz)
    )
    gap = lax.broadcasted_iota(jnp.int32, (nz, nz), 0) - lax.broadcasted_iota(
        jnp.int32, (nz, nz), 1
    )
    for forward in (0, 1):
        band = jnp.zeros((nz, nz), jnp.float32)
        for k in range(1, 5):
            later, earlier = (k, 1 - k) if forward else (k - 1, -k)
            band = jnp.where(gap == later, coeffs[k - 1], band)
            band = jnp.where(gap == earlier, -coeffs[k - 1], band)
        bands[forward] = band

    def locate(cells):
        cell_x = quotient(cells, ny * wy * nz)
        cell_y = remainder(quotient(cells, nz), ny * wy)
        near_x = cell_x - gx * wx
        near_y = cell_y - gy * wy
        inside = (near_x >= 0) & (near_x < wx) & (near_y >= 0) & (near_y < wy)
        return jnp.where(inside, near_x * wy + near_y, -1), remainder(cells, nz)

    def match(indices, count):
        wide = (count, indices.shape[1])
        return jnp.where(lax.broadcasted_iota(jnp.int32, wide, 0) == indices, 1.0, 0.0).astype(
            jnp.float32
        )

    row, deep = locate(source_ref[...])
    source_row = match(row, wx * wy)
    source_z[...] = match(deep, nz)
    row, deep = locate(probe_ref[...])
    probe_row[...] = match(row, wx * wy)
    probe_z[...] = match(deep, nz)
    for t in range(steps):
        push[t] = lax.dot_general(
            source_row * (time_step * amps_ref[t : t + 1, :]),
            source_z[...],
            (((1,), (1,)), ((), ())),
            precision=EXACT,
            preferred_element_type=jnp.float32,
        ).reshape(wx, wy, nz)

    for f in (SZZ, VY, VX, VZ):
        loads[f].wait()

    def put(f, value):
        F[f, LX, LY, :] = value

    def get(f):
        return F[f, LX, LY, :]

    def step(t, carry):
        fade = jnp.where(t == 0, 1.0, damp[...])
        z_y = depth(SYZ, False)
        z_x = depth(SXZ, False)
        z_z = depth(SZZ, True)
        arrived((SXY, 0), (SYY, 1))
        put(VY, fade * get(VY) + buoy[...] * (along(SXY, 0) + along(SYY, 1) + z_y))
        send((VY, 0), (VY, 1))
        arrived((SXX, 0), (SXY, 1))
        put(VX, fade * get(VX) + buoy[...] * (along(SXX, 0) + along(SXY, 1) + z_x))
        send((VX, 0), (VX, 1))
        arrived((SXZ, 0), (SYZ, 1))
        put(VZ, fade * get(VZ) + buoy[...] * (along(SXZ, 0) + along(SYZ, 1) + z_z))
        send((VZ, 0), (VZ, 1))

        z_z = depth(VZ, False)
        z_x = depth(VX, True)
        z_y = depth(VY, True)
        sent(*stress_keys)
        arrived((VY, 0), (VX, 1))
        put(SXY, damp[...] * (get(SXY) + shear[...] * (along(VX, 1) + along(VY, 0))))

        @pl.when(t < steps - 1)
        def _():
            send((SXY, 0), (SXY, 1))

        arrived((VX, 0), (VY, 1))
        e_x, e_y, e_z = along(VX, 0), along(VY, 1), z_z
        base = lame[...] * (e_x + e_y + e_z) + push[t]
        twice = 2.0 * shear[...]
        n_x = damp[...] * (get(SXX) + (base + twice * e_x))
        n_y = damp[...] * (get(SYY) + (base + twice * e_y))
        n_z = damp[...] * (get(SZZ) + (base + twice * e_z))
        put(SXX, n_x)
        put(SYY, n_y)
        put(SZZ, n_z)
        press[...] = -(n_x + n_y + n_z) / 3.0

        @pl.when(t < steps - 1)
        def _():
            send((SXX, 0), (SYY, 1))

        arrived((VZ, 0), (VZ, 1))
        put(SXZ, damp[...] * (get(SXZ) + shear[...] * (z_x + along(VZ, 0))))
        put(SYZ, damp[...] * (get(SYZ) + shear[...] * (z_y + along(VZ, 1))))

        @pl.when(t < steps - 1)
        def _():
            send((SXZ, 0), (SYZ, 1))

        picked = jnp.dot(
            press[...].reshape(wx * wy, nz), probe_z[...],
            precision=EXACT, preferred_element_type=jnp.float32,
        )
        rows_y[0, pl.ds(t, 1), :] = jnp.sum(picked * probe_row[...], axis=0, keepdims=True)
        sent(*speed_keys)
        return carry

    lax.fori_loop(0, steps, step, 0)

    def gather(axis, buffer, ssem, rsem):
        n = extent[axis]
        copies = [
            pltpu.make_async_remote_copy(
                src_ref=buffer.at[0], dst_ref=buffer.at[d],
                send_sem=ssem.at[d], recv_sem=rsem.at[d],
                device_id={axis_name[axis]: lax.rem(place[axis] + d, n)},
                device_id_type=pl.DeviceIdType.MESH,
            )
            for d in range(1, n)
        ]
        for one in copies:
            one.start()
        return copies

    def total(buffer):
        value = buffer[0]
        for d in range(1, buffer.shape[0]):
            value = value + buffer[d]
        return value

    first = gather(1, rows_y, tsend_y, trecv_y)
    for f in (SXX, SYY, SZZ, SXY, SXZ, SYZ):
        out_ref[f] = get(f)
    for one in first:
        one.wait_recv()
    rows_x[0] = total(rows_y)
    second = gather(0, rows_x, tsend_x, trecv_x)
    for f in (VX, VY, VZ):
        out_ref[f] = damp[...] * get(f)
    for one in second:
        one.wait_recv()
    traces_ref[...] = total(rows_x)[:steps]
    for one in first + second:
        one.wait_send()


def body(nx, ny, wavefield, labels, lame, shear, density, source_cells, source_amps, receiver_cells):
    _, wx, wy, nz = wavefield.shape
    steps, sources = source_amps.shape
    probes = receiver_cells.shape[0]
    padded = -(-steps // 8) * 8
    cells = (wx, wy, nz)
    vmem = pl.BlockSpec(memory_space=pltpu.VMEM)
    smem = pl.BlockSpec(memory_space=pltpu.SMEM)
    anywhere = pl.BlockSpec(memory_space=pl.ANY)
    f32 = jnp.float32
    return pl.pallas_call(
        functools.partial(kernel, (nx, ny, steps)),
        out_shape=(
            jax.ShapeDtypeStruct(wavefield.shape, f32),
            jax.ShapeDtypeStruct((steps, probes), f32),
        ),
        in_specs=[anywhere, anywhere, smem, smem, smem, vmem, vmem, vmem],
        out_specs=(vmem, vmem),
        scratch_shapes=[
            pltpu.VMEM((9, wx + 2 * RIM_X, wy + 2 * RIM_Y, nz), f32),
            pltpu.VMEM(cells, jnp.int32),
            pltpu.VMEM(cells, f32),
            pltpu.VMEM(cells, f32),
            pltpu.VMEM(cells, f32),
            pltpu.VMEM(cells, f32),
            pltpu.VMEM((2, nz, nz), f32),
            pltpu.VMEM((nz, sources), f32),
            pltpu.VMEM((nz, probes), f32),
            pltpu.VMEM((wx * wy, probes), f32),
            pltpu.VMEM((steps,) + cells, f32),
            pltpu.VMEM(cells, f32),
            pltpu.VMEM((ny, padded, probes), f32),
            pltpu.VMEM((nx, padded, probes), f32),
            pltpu.SemaphoreType.DMA((10,)),
            pltpu.SemaphoreType.DMA((len(EXCHANGED), 2)),
            pltpu.SemaphoreType.DMA((len(EXCHANGED), 2)),
            pltpu.SemaphoreType.DMA((ny,)),
            pltpu.SemaphoreType.DMA((ny,)),
            pltpu.SemaphoreType.DMA((nx,)),
            pltpu.SemaphoreType.DMA((nx,)),
        ],
        compiler_params=pltpu.CompilerParams(
            collective_id=0, has_side_effects=True, vmem_limit_bytes=24 * 1024 * 1024
        ),
    )(
        wavefield, labels, lame, shear, density,
        source_cells.reshape(1, sources), source_amps, receiver_cells.reshape(1, probes),
    )


def solution(mesh):
    field = P(None, ("shot", "gx"), "gy", None)
    placed = (field, P("gx", "gy", None), P(), P(), P(), P("shot"), P(None, "shot"), P())
    return jax.shard_map(
        functools.partial(body, mesh.shape["gx"], mesh.shape["gy"]),
        mesh=mesh,
        in_specs=placed,
        out_specs=(field, P(None, "shot")),
        check_vma=False,
    )
```

profile of v0, /device:TPU:0, one launch (start us, length us, event | category | flops | bytes accessed | tf_op | source)
XLA Modules:
  0.0 50.3 jit_solution(2792491761395158307)
XLA Ops:
  0.6 0.0 copy-start.5
  0.6 0.0 copy-start.6
  0.7 0.0 copy-start.7
  0.7 0.0 copy-start.3
  0.7 0.0 copy-start.4
  0.7 0.6 %copy-done.5 = f32[8]{0:T(128)S(1)} copy-done((f32[8]{0:T(128)S(1)}, f32[8]{0:T(128)}, u32[]{:S(2)}) %copy-start.5) | copy-done | bytes 56
  1.3 0.0 copy-done.6
  1.3 0.0 copy-done.7
  1.3 0.0 copy-done.3
  1.4 0.0 copy-done.4
  1.4 0.0 copy-start
  1.4 1.1 %copy-done = f32[9,8,16,128]{3,2,1,0:T(8,128)S(1)} copy-done((f32[9,8,16,128]{3,2,1,0:T(8,128)S(1)}, f32[9,8,16,128]{3,2,1,0:T(8,128)}, u32[]{:S(2)}) %copy-start) | copy-done | bytes 589848
  2.4 0.0 copy-start.1
  2.4 0.8 %copy-done.1 = s32[8,16,128]{2,1,0:T(8,128)S(1)} copy-done((s32[8,16,128]{2,1,0:T(8,128)S(1)}, s32[8,16,128]{2,1,0:T(8,128)}, u32[]{:S(2)}) %copy-start.1) | copy-done | bytes 65560
  3.3 0.0 copy-start.2
  3.3 0.7 %copy-done.2 = f32[5,64]{1,0:T(8,128)S(1)} copy-done((f32[5,64]{1,0:T(8,128)S(1)}, f32[5,64]{1,0:T(8,128)}, u32[]{:S(2)}) %copy-start.2) | copy-done | bytes 1304
  4.0 44.9 %shard_map.95 = (f32[9,8,16,128]{3,2,1,0:T(8,128)S(1)}, f32[5,256]{1,0:T(8,128)S(1)}) custom-call(f32[9,8,16,128]{3,2,1,0:T(8,128)S(1)} %copy-done, s32[8,16,128]{2,1,0:T(8,128)S(1)} %copy-done.1, f32[8]{0:T(128)S(1)} %copy-done.4, f32[8]{0:T(128)S(1)} %copy-done.5, f32[8]{0:T(128)S(1)} %copy-done.6, s32[1,64]{1,0:T(1,128)S(1)} %bitcast.3, ...), custom_call_target="tpu_custom_call" | custom-call | tf_op jit(solution)/shard_map/pallas_call | solution.py:355
  48.9 0.8 %copy.12 = f32[9,8,16,128]{3,2,1,0:T(8,128)} copy(f32[9,8,16,128]{3,2,1,0:T(8,128)S(1)} %get-tuple-element.4) | data formatting | bytes 1179648
  49.7 0.6 %copy.13 = f32[5,256]{1,0:T(8,128)} copy(f32[5,256]{1,0:T(8,128)S(1)} %get-tuple-element.5) | data formatting | bytes 10240
Async XLA Ops:
  0.6 0.7 %copy-start.5 = (f32[8]{0:T(128)S(1)}, f32[8]{0:T(128)}, u32[]{:S(2)}) copy-start(f32[8]{0:T(128)} %shear_ref.1) | copy-start | bytes 100
  0.6 0.7 %copy-start.6 = (f32[8]{0:T(128)S(1)}, f32[8]{0:T(128)}, u32[]{:S(2)}) copy-start(f32[8]{0:T(128)} %density_ref.1) | copy-start | bytes 100
  0.7 0.7 %copy-start.7 = (s32[64]{0:T(128)S(1)}, s32[64]{0:T(128)}, u32[]{:S(2)}) copy-start(s32[64]{0:T(128)} %param.13) | copy-start | bytes 772
  0.7 0.7 %copy-start.3 = (s32[256]{0:T(256)S(1)}, s32[256]{0:T(256)}, u32[]{:S(2)}) copy-start(s32[256]{0:T(256)} %param.15) | copy-start | bytes 3076
  0.7 0.7 %copy-start.4 = (f32[8]{0:T(128)S(1)}, f32[8]{0:T(128)}, u32[]{:S(2)}) copy-start(f32[8]{0:T(128)} %lame_ref.1) | copy-start | bytes 100
  1.4 1.1 %copy-start = (f32[9,8,16,128]{3,2,1,0:T(8,128)S(1)}, f32[9,8,16,128]{3,2,1,0:T(8,128)}, u32[]{:S(2)}) copy-start(f32[9,8,16,128]{3,2,1,0:T(8,128)} %wave_ref.1) | copy-start | bytes 1769476
  2.4 0.8 %copy-start.1 = (s32[8,16,128]{2,1,0:T(8,128)S(1)}, s32[8,16,128]{2,1,0:T(8,128)}, u32[]{:S(2)}) copy-start(s32[8,16,128]{2,1,0:T(8,128)} %labels_ref.1) | copy-start | bytes 196612
  3.3 0.7 %copy-start.2 = (f32[5,64]{1,0:T(8,128)S(1)}, f32[5,64]{1,0:T(8,128)}, u32[]{:S(2)}) copy-start(f32[5,64]{1,0:T(8,128)} %amps_ref.1) | copy-start | bytes 3844
where the time goes:
time: 50.5 us; the launch traced here: 50.3 us
  Pallas kernels  44.9 us (89%)
  local copies, waits for them, and re-layouts  4.69 us (9%)
  between operations  0.69 us (1%)
    pallas_call x1, Pallas kernels, body(): pl.pallas_call(functools.partial(kernel, (nx, ny, steps)), out_shape=(jax...  44.9 us
    unnamed x18, local copies, waits for them, and re-layouts  4.69 us

commit v1 on v0

--- a/solution.py
+++ b/solution.py
@@ -21,6 +21,7 @@
 SLOT = {key: number for number, key in enumerate(EXCHANGED)}
 RIM_X = 4
 RIM_Y = 8
+LIMIT = 24 * 1024 * 1024
 EXACT = lax.Precision.HIGHEST
 
 
@@ -47,6 +48,7 @@
     wave_ref, labels_ref, lame_ref, shear_ref, density_ref,
     source_ref, amps_ref, probe_ref,
     out_ref, traces_ref,
+    lame_table, shear_table, density_table, sources, amps, probes,
     F, labels, lame, shear, buoy, damp, bands, source_z, probe_z, probe_row, push, press,
     rows_y, rows_x,
     load_sem, send_sem, recv_sem, tsend_y, trecv_y, tsend_x, trecv_x,
@@ -66,9 +68,18 @@
         pltpu.make_async_copy(wave_ref.at[f], local(f), load_sem.at[f]) for f in range(9)
     ]
     load_labels = pltpu.make_async_copy(labels_ref, labels, load_sem.at[9])
+    small = [
+        pltpu.make_async_copy(source, sink, load_sem.at[10 + number])
+        for number, (source, sink) in enumerate((
+            (lame_ref, lame_table), (shear_ref, shear_table), (density_ref, density_table),
+            (source_ref, sources), (amps_ref, amps), (probe_ref, probes),
+        ))
+    ]
     for f in (SXY, SXX, SXZ, SYY, SYZ):
         loads[f].start()
     load_labels.start()
+    for one in small:
+        one.start()
     for f in (SZZ, VY, VX, VZ):
         loads[f].start()
 
@@ -179,6 +190,8 @@
     send(*stress_keys)
 
     load_labels.wait()
+    for one in small:
+        one.wait()
     tissue = labels[...]
 
     def lookup(table):
@@ -187,9 +200,9 @@
             value = jnp.where(tissue == number, table[number], value)
         return value
 
-    lame[...] = time_step * lookup(lame_ref)
-    shear[...] = time_step * lookup(shear_ref)
-    buoy[...] = time_step / lookup(density_ref)
+    lame[...] = time_step * lookup(lame_table)
+    shear[...] = time_step * lookup(shear_table)
+    buoy[...] = time_step / lookup(density_table)
     shape = (wx, wy, nz)
     damp[...] = (
         profile(gx * wx + lax.broadcasted_iota(jnp.int32, shape, 0), nx * wx)
@@ -221,15 +234,15 @@
             jnp.float32
         )
 
-    row, deep = locate(source_ref[...])
+    row, deep = locate(sources[...])
     source_row = match(row, wx * wy)
     source_z[...] = match(deep, nz)
-    row, deep = locate(probe_ref[...])
+    row, deep = locate(probes[...])
     probe_row[...] = match(row, wx * wy)
     probe_z[...] = match(deep, nz)
     for t in range(steps):
         push[t] = lax.dot_general(
-            source_row * (time_step * amps_ref[t : t + 1, :]),
+            source_row * (time_step * amps[t : t + 1, :]),
             source_z[...],
             (((1,), (1,)), ((), ())),
             precision=EXACT,
@@ -244,6 +257,28 @@
 
     def get(f):
         return F[f, LX, LY, :]
+
+    def gather(axis, buffer, ssem, rsem):
+        n = extent[axis]
+        copies = [
+            pltpu.make_async_remote_copy(
+                src_ref=buffer.at[0], dst_ref=buffer.at[d],
+                send_sem=ssem.at[d], recv_sem=rsem.at[d],
+                device_id={axis_name[axis]: lax.rem(place[axis] + d, n)},
+                device_id_type=pl.DeviceIdType.MESH,
+            )
+            for d in range(1, n)
+        ]
+        return copies
+
+    def total(buffer):
+        value = buffer[0]
+        for d in range(1, buffer.shape[0]):
+            value = value + buffer[d]
+        return value
+
+    first = gather(1, rows_y, tsend_y, trecv_y)
+    second = gather(0, rows_x, tsend_x, trecv_x)
 
     def step(t, carry):
         fade = jnp.where(t == 0, 1.0, damp[...])
@@ -287,59 +322,51 @@
         def _():
             send((SXX, 0), (SYY, 1))
 
-        arrived((VZ, 0), (VZ, 1))
-        put(SXZ, damp[...] * (get(SXZ) + shear[...] * (z_x + along(VZ, 0))))
-        put(SYZ, damp[...] * (get(SYZ) + shear[...] * (z_y + along(VZ, 1))))
-
-        @pl.when(t < steps - 1)
-        def _():
-            send((SXZ, 0), (SYZ, 1))
-
         picked = jnp.dot(
             press[...].reshape(wx * wy, nz), probe_z[...],
             precision=EXACT, preferred_element_type=jnp.float32,
         )
         rows_y[0, pl.ds(t, 1), :] = jnp.sum(picked * probe_row[...], axis=0, keepdims=True)
+
+        @pl.when(t == steps - 1)
+        def _():
+            for one in first:
+                one.start()
+
+        arrived((VZ, 0), (VZ, 1))
+        put(SXZ, damp[...] * (get(SXZ) + shear[...] * (z_x + along(VZ, 0))))
+        put(SYZ, damp[...] * (get(SYZ) + shear[...] * (z_y + along(VZ, 1))))
+
+        @pl.when(t < steps - 1)
+        def _():
+            send((SXZ, 0), (SYZ, 1))
+
         sent(*speed_keys)
         return carry
 
     lax.fori_loop(0, steps, step, 0)
 
-    def gather(axis, buffer, ssem, rsem):
-        n = extent[axis]
-        copies = [
-            pltpu.make_async_remote_copy(
-                src_ref=buffer.at[0], dst_ref=buffer.at[d],
-                send_sem=ssem.at[d], recv_sem=rsem.at[d],
-                device_id={axis_name[axis]: lax.rem(place[axis] + d, n)},
-                device_id_type=pl.DeviceIdType.MESH,
-            )
-            for d in range(1, n)
-        ]
-        for one in copies:
-            one.start()
-        return copies
-
-    def total(buffer):
-        value = buffer[0]
-        for d in range(1, buffer.shape[0]):
-            value = value + buffer[d]
-        return value
-
-    first = gather(1, rows_y, tsend_y, trecv_y)
+    stores = [
+        pltpu.make_async_copy(local(f), out_ref.at[f], load_sem.at[f]) for f in range(9)
+    ]
     for f in (SXX, SYY, SZZ, SXY, SXZ, SYZ):
-        out_ref[f] = get(f)
+        stores[f].start()
+    for f in (VX, VY, VZ):
+        put(f, damp[...] * get(f))
+    for f in (VX, VY, VZ):
+        stores[f].start()
     for one in first:
         one.wait_recv()
     rows_x[0] = total(rows_y)
-    second = gather(0, rows_x, tsend_x, trecv_x)
-    for f in (VX, VY, VZ):
-        out_ref[f] = damp[...] * get(f)
+    for one in second:
+        one.start()
     for one in second:
         one.wait_recv()
     traces_ref[...] = total(rows_x)[:steps]
     for one in first + second:
         one.wait_send()
+    for one in stores:
+        one.wait()
 
 
 def body(nx, ny, wavefield, labels, lame, shear, density, source_cells, source_amps, receiver_cells):
@@ -349,8 +376,6 @@
     padded = -(-steps // 8) * 8
     cells = (wx, wy, nz)
     vmem = pl.BlockSpec(memory_space=pltpu.VMEM)
-    smem = pl.BlockSpec(memory_space=pltpu.SMEM)
-    anywhere = pl.BlockSpec(memory_space=pl.ANY)
     f32 = jnp.float32
     return pl.pallas_call(
         functools.partial(kernel, (nx, ny, steps)),
@@ -358,9 +383,15 @@
             jax.ShapeDtypeStruct(wavefield.shape, f32),
             jax.ShapeDtypeStruct((steps, probes), f32),
         ),
-        in_specs=[anywhere, anywhere, smem, smem, smem, vmem, vmem, vmem],
+        in_specs=[pl.BlockSpec(memory_space=pltpu.HBM)] * 8,
         out_specs=(vmem, vmem),
         scratch_shapes=[
+            pltpu.SMEM(lame.shape, f32),
+            pltpu.SMEM(shear.shape, f32),
+            pltpu.SMEM(density.shape, f32),
+            pltpu.VMEM((1, sources), jnp.int32),
+            pltpu.VMEM((steps, sources), f32),
+            pltpu.VMEM((1, probes), jnp.int32),
             pltpu.VMEM((9, wx + 2 * RIM_X, wy + 2 * RIM_Y, nz), f32),
             pltpu.VMEM(cells, jnp.int32),
             pltpu.VMEM(cells, f32),
@@ -375,7 +406,7 @@
             pltpu.VMEM(cells, f32),
             pltpu.VMEM((ny, padded, probes), f32),
             pltpu.VMEM((nx, padded, probes), f32),
-            pltpu.SemaphoreType.DMA((10,)),
+            pltpu.SemaphoreType.DMA((16,)),
             pltpu.SemaphoreType.DMA((len(EXCHANGED), 2)),
             pltpu.SemaphoreType.DMA((len(EXCHANGED), 2)),
             pltpu.SemaphoreType.DMA((ny,)),
@@ -384,11 +415,16 @@
             pltpu.SemaphoreType.DMA((nx,)),
         ],
         compiler_params=pltpu.CompilerParams(
-            collective_id=0, has_side_effects=True, vmem_limit_bytes=24 * 1024 * 1024
+            collective_id=0, has_side_effects=True, vmem_limit_bytes=LIMIT
         ),
     )(
-        wavefield, labels, lame, shear, density,
-        source_cells.reshape(1, sources), source_amps, receiver_cells.reshape(1, probes),
+        *(
+            pltpu.with_memory_space_constraint(value, pltpu.HBM)
+            for value in (
+                wavefield, labels, lame, shear, density,
+                source_cells.reshape(1, sources), source_amps, receiver_cells.reshape(1, probes),
+            )
+        )
     )
 
 

time: 50.5 us -> 45.3 us (0.90)
  local copies, waits for them, and re-layouts: 4.69 us -> 1.42 us
  Pallas kernels: 44.9 us -> 43.1 us
    unnamed x18 -> x2, local copies, waits for them, and re-layouts: 4.69 us -> 1.42 us
    pallas_call x1, Pallas kernels: 44.9 us -> 43.1 us  [body(): pl.pallas_call(functools.partial(kernel, (nx, ny, steps)), out_shape=(jax...]
where the time goes in v1:
time: 45.3 us; the launch traced here: 45.2 us
  Pallas kernels  43.1 us (95%)
  local copies, waits for them, and re-layouts  1.42 us (3%)
  between operations  0.64 us (1%)
    pallas_call x1, Pallas kernels, body(): pl.pallas_call(functools.partial(kernel, (nx, ny, steps)), out_shape=(jax...  43.1 us
    unnamed x2, local copies, waits for them, and re-layouts  1.42 us

profile of v1, /device:TPU:0, one launch (start us, length us, event | category | flops | bytes accessed | tf_op | source)
XLA Modules:
  0.0 45.2 jit_solution(10792832270234731784)
XLA Ops:
  0.6 43.1 %shard_map.95 = (f32[9,8,16,128]{3,2,1,0:T(8,128)S(1)}, f32[5,256]{1,0:T(8,128)S(1)}) custom-call(f32[9,8,16,128]{3,2,1,0:T(8,128)} %wave_ref.1, s32[8,16,128]{2,1,0:T(8,128)} %labels_ref.1, f32[8]{0:T(128)} %lame_ref.1, f32[8]{0:T(128)} %shear_ref.1, f32[8]{0:T(128)} %density_ref.1, s32[1,64]{1,0:T(1,128)} %bitcast.3, f32[5,64]{1,0:T(8,128)} %amps_ref.1, ...), custom_call_target="tpu_custom_call" | custom-call | tf_op jit(solution)/shard_map/pallas_call | solution.py:380
  43.8 0.8 %copy.12 = f32[9,8,16,128]{3,2,1,0:T(8,128)} copy(f32[9,8,16,128]{3,2,1,0:T(8,128)S(1)} %get-tuple-element.4) | data formatting | bytes 1179648
  44.6 0.6 %copy.13 = f32[5,256]{1,0:T(8,128)} copy(f32[5,256]{1,0:T(8,128)S(1)} %get-tuple-element.5) | data formatting | bytes 10240

commit v2 on v1

--- a/solution.py
+++ b/solution.py
@@ -50,7 +50,7 @@
     out_ref, traces_ref,
     lame_table, shear_table, density_table, sources, amps, probes,
     F, labels, lame, shear, buoy, damp, bands, source_z, probe_z, probe_row, push, press,
-    rows_y, rows_x,
+    rows_y, rows_x, last, lsend, lrecv,
     load_sem, send_sem, recv_sem, tsend_y, trecv_y, tsend_x, trecv_x,
 ):
     nx, ny, steps = sizes
@@ -93,14 +93,16 @@
     rows_y[...] = jnp.zeros(rows_y.shape, jnp.float32)
 
     barrier = pltpu.get_barrier_semaphore()
-    for axis in (0, 1):
-        for d in range(1, extent[axis]):
-            pl.semaphore_signal(
-                barrier, inc=1,
-                device_id={axis_name[axis]: lax.rem(place[axis] + d, extent[axis])},
-                device_id_type=pl.DeviceIdType.MESH,
-            )
-    pl.semaphore_wait(barrier, nx + ny - 2)
+    peers = [(a, b) for a in range(nx) for b in range(ny) if a + b > 0]
+
+    def peer(a, b):
+        return {"gx": lax.rem(gx + a, nx), "gy": lax.rem(gy + b, ny)}
+
+    for a, b in peers:
+        pl.semaphore_signal(
+            barrier, inc=1, device_id=peer(a, b), device_id_type=pl.DeviceIdType.MESH
+        )
+    pl.semaphore_wait(barrier, len(peers))
 
     def copy(f, axis, up):
         forward = EXCHANGED[f, axis]
@@ -277,6 +279,14 @@
             value = value + buffer[d]
         return value
 
+    spread = [
+        pltpu.make_async_remote_copy(
+            src_ref=last.at[0], dst_ref=last.at[a * ny + b],
+            send_sem=lsend.at[a * ny + b], recv_sem=lrecv.at[a * ny + b],
+            device_id=peer(a, b), device_id_type=pl.DeviceIdType.MESH,
+        )
+        for a, b in peers
+    ]
     first = gather(1, rows_y, tsend_y, trecv_y)
     second = gather(0, rows_x, tsend_x, trecv_x)
 
@@ -295,6 +305,14 @@
         put(VZ, fade * get(VZ) + buoy[...] * (along(SXZ, 0) + along(SYZ, 1) + z_z))
         send((VZ, 0), (VZ, 1))
 
+        @pl.when(t == steps - 1)
+        def _():
+            for one in first:
+                one.wait_recv()
+            rows_x[0] = total(rows_y)
+            for one in second:
+                one.start()
+
         z_z = depth(VZ, False)
         z_x = depth(VX, True)
         z_y = depth(VY, True)
@@ -326,11 +344,16 @@
             press[...].reshape(wx * wy, nz), probe_z[...],
             precision=EXACT, preferred_element_type=jnp.float32,
         )
-        rows_y[0, pl.ds(t, 1), :] = jnp.sum(picked * probe_row[...], axis=0, keepdims=True)
+        line = jnp.sum(picked * probe_row[...], axis=0, keepdims=True)
+
+        @pl.when(t < steps - 1)
+        def _():
+            rows_y[0, pl.ds(t, 1), :] = line
 
         @pl.when(t == steps - 1)
         def _():
-            for one in first:
+            last[0] = line
+            for one in spread:
                 one.start()
 
         arrived((VZ, 0), (VZ, 1))
@@ -340,6 +363,11 @@
         @pl.when(t < steps - 1)
         def _():
             send((SXZ, 0), (SYZ, 1))
+
+        @pl.when(t == steps - 2)
+        def _():
+            for one in first:
+                one.start()
 
         sent(*speed_keys)
         return carry
@@ -355,15 +383,13 @@
         put(f, damp[...] * get(f))
     for f in (VX, VY, VZ):
         stores[f].start()
-    for one in first:
-        one.wait_recv()
-    rows_x[0] = total(rows_y)
-    for one in second:
-        one.start()
     for one in second:
         one.wait_recv()
+    for one in spread:
+        one.wait_recv()
     traces_ref[...] = total(rows_x)[:steps]
-    for one in first + second:
+    traces_ref[steps - 1 : steps, :] = total(last)
+    for one in first + second + spread:
         one.wait_send()
     for one in stores:
         one.wait()
@@ -406,6 +432,9 @@
             pltpu.VMEM(cells, f32),
             pltpu.VMEM((ny, padded, probes), f32),
             pltpu.VMEM((nx, padded, probes), f32),
+            pltpu.VMEM((nx * ny, 1, probes), f32),
+            pltpu.SemaphoreType.DMA((nx * ny,)),
+            pltpu.SemaphoreType.DMA((nx * ny,)),
             pltpu.SemaphoreType.DMA((16,)),
             pltpu.SemaphoreType.DMA((len(EXCHANGED), 2)),
             pltpu.SemaphoreType.DMA((len(EXCHANGED), 2)),

time: 45.3 us -> 44.9 us (level)
  no operation moved by 1% of the time
where the time goes in v2:
time: 44.9 us; the launch traced here: 44.8 us
  Pallas kernels  42.7 us (95%)
  local copies, waits for them, and re-layouts  1.42 us (3%)
  between operations  0.64 us (1%)
    pallas_call x1, Pallas kernels, body(): pl.pallas_call(functools.partial(kernel, (nx, ny, steps)), out_shape=(jax...  42.7 us
    unnamed x2, local copies, waits for them, and re-layouts  1.42 us

profile of v2, /device:TPU:0, one launch (start us, length us, event | category | flops | bytes accessed | tf_op | source)
XLA Modules:
  0.0 44.8 jit_solution(4267524384976117810)
XLA Ops:
  0.6 42.7 %shard_map.95 = (f32[9,8,16,128]{3,2,1,0:T(8,128)S(1)}, f32[5,256]{1,0:T(8,128)S(1)}) custom-call(f32[9,8,16,128]{3,2,1,0:T(8,128)} %wave_ref.1, s32[8,16,128]{2,1,0:T(8,128)} %labels_ref.1, f32[8]{0:T(128)} %lame_ref.1, f32[8]{0:T(128)} %shear_ref.1, f32[8]{0:T(128)} %density_ref.1, s32[1,64]{1,0:T(1,128)} %bitcast.3, f32[5,64]{1,0:T(8,128)} %amps_ref.1, ...), custom_call_target="tpu_custom_call" | custom-call | tf_op jit(solution)/shard_map/pallas_call | solution.py:406
  43.3 0.8 %copy.12 = f32[9,8,16,128]{3,2,1,0:T(8,128)} copy(f32[9,8,16,128]{3,2,1,0:T(8,128)S(1)} %get-tuple-element.4) | data formatting | bytes 1179648
  44.2 0.6 %copy.13 = f32[5,256]{1,0:T(8,128)} copy(f32[5,256]{1,0:T(8,128)S(1)} %get-tuple-element.5) | data formatting | bytes 10240
